TPU v7x, 32 devices: a whole 2x2x4 slice. The times are simulated.
32 devices in a mesh: dp: 8 (over y, x, core), fsdp: 4 (over z).
Axes of the slice: x: 2, y: 2, z: 4, core: 2. Of those that a mesh axis runs over, the one named last changes fastest.
Arguments:
- tokens: bfloat16 [4096, 4096], P('dp'), may hold values from -6 to 6
- counts: int32 [8], P('dp'), may hold values from 256 to 512, as said below
- patch_index: int32 [4096], P('dp'), may hold values from 0 to 255
- clip_limit: float32 [], replicated, may hold values from 1024 to 8192
- norm_gain: float32 [4, 4096], replicated, may hold values from 0.25 to 1.75
- params: float32 [4, 4096, 4096], P(None, 'dp', 'fsdp'), may hold values from -0.09375 to 0.09375
- moments: float32 [4, 4096, 4096], P(None, 'dp', 'fsdp'), may hold values from -0.3 to 0.3
- seconds: float32 [4, 4096, 4096], P(None, 'dp', 'fsdp'), may hold values from 0.05 to 1
- gradients: float32 [4, 4096, 4096], P(None, 'dp', 'fsdp'), may hold values from -48 to 48
Outputs:
- params_new: float32 [4, 4096, 4096], P(None, 'dp', 'fsdp')
- moments_new: float32 [4, 4096, 4096], P(None, 'dp', 'fsdp')
- seconds_new: float32 [4, 4096, 4096], P(None, 'dp', 'fsdp')
- mixed: bfloat16 [4096, 4096], P('dp', 'fsdp')
Inputs may be any that keep to these rules, and one draw needn't show every extreme that they name: `counts`: at most 512, reached on some index of dp in every draw.
All inputs are finite; a program needn't handle non-finite values.
Results may differ from a plain program's by a relative error of at most 0.0095.
Values may be sent and summed in bfloat16 or wider, within the bound.
A program may use at most 192 MiB of HBM per device.

v0:
```python
import jax
import jax.numpy as jnp
from jax import lax
from jax.sharding import PartitionSpec as P

D = 4096
LAYERS = 4
GRID = 16
STEP = 40
beta_one = 0.9
beta_two = 0.95
adam_eps = 1e-08
learning_rate = 0.0024
weight_decay = 0.05
norm_eps = 1e-06


def position_code(patch_index):
    quarter = D // 4
    freqs = 1.0 / 10000.0 ** (jnp.arange(quarter, dtype=jnp.float32) / quarter)
    across = (patch_index // GRID).astype(jnp.float32)[:, None] * freqs[None, :]
    downward = (patch_index % GRID).astype(jnp.float32)[:, None] * freqs[None, :]
    return jnp.concatenate(
        [jnp.sin(across), jnp.cos(across), jnp.sin(downward), jnp.cos(downward)], axis=1
    )


def layer_norm(stream, gain_row):
    centre = jnp.mean(stream, axis=1, keepdims=True)
    shifted = stream - centre
    spread = jnp.mean(shifted * shifted, axis=1, keepdims=True)
    return (shifted * lax.rsqrt(spread + norm_eps) * gain_row[None, :]).astype(jnp.bfloat16)


def adam_update(params, moments, seconds, gradients, factor):
    clipped = gradients * factor
    moments_new = beta_one * moments + (1.0 - beta_one) * clipped
    seconds_new = beta_two * seconds + (1.0 - beta_two) * clipped * clipped
    direction = (
        moments_new
        / (1.0 - beta_one**STEP)
        / (jnp.sqrt(seconds_new / (1.0 - beta_two**STEP)) + adam_eps)
    )
    params_new = params - learning_rate * (direction + weight_decay * params)
    return (params_new, moments_new, seconds_new)


def advance(stream, branch, current, col_first, col_count):
    if current + 1 < LAYERS:
        widened = lax.all_gather(branch, "fsdp", axis=1, tiled=True)
        return stream + widened.astype(jnp.float32)
    return lax.dynamic_slice_in_dim(stream, col_first, col_count, 1) + branch.astype(jnp.float32)


def per_device(
    tokens, counts, patch_index, clip_limit, norm_gain, params, moments, seconds, gradients
):
    squares = lax.psum(jnp.sum(gradients * gradients), ("dp", "fsdp"))
    factor = jnp.minimum(1.0, clip_limit / (jnp.sqrt(squares) + 1e-06))
    params_new, moments_new, seconds_new = adam_update(params, moments, seconds, gradients, factor)
    weights = params_new.astype(jnp.bfloat16)
    tok_rows = tokens.shape[0]
    col_count = weights.shape[2]
    col_first = lax.axis_index("fsdp") * col_count
    valid = lax.broadcasted_iota(jnp.int32, (tok_rows, 1), 0) < counts[0]
    stream = jnp.where(valid, tokens.astype(jnp.float32) + position_code(patch_index), 0.0)
    gathered = lax.all_gather(weights, "dp", axis=1, tiled=True)
    for current in range(LAYERS):
        normed = layer_norm(stream, norm_gain[current])
        branch = jnp.dot(normed, gathered[current], preferred_element_type=jnp.float32).astype(
            jnp.bfloat16
        )
        stream = advance(stream, branch, current, col_first, col_count)
    mixed = jnp.where(valid, stream, 0.0).astype(jnp.bfloat16)
    return (params_new, moments_new, seconds_new, mixed)


def solution(mesh):
    in_specs = (
        P("dp", None),
        P("dp"),
        P("dp"),
        P(),
        P(),
        P(None, "dp", "fsdp"),
        P(None, "dp", "fsdp"),
        P(None, "dp", "fsdp"),
        P(None, "dp", "fsdp"),
    )
    out_specs = (
        P(None, "dp", "fsdp"),
        P(None, "dp", "fsdp"),
        P(None, "dp", "fsdp"),
        P("dp", "fsdp"),
    )
    return jax.shard_map(
        per_device, mesh=mesh, in_specs=in_specs, out_specs=out_specs, check_vma=False
    )
```

profile of v0, /device:TPU:0, one launch (start us, length us, event | category | flops | bytes accessed | tf_op | source)
XLA Modules:
  0.0 556.9 jit_solution(18285389573598532073)
XLA Ops:
  7.2 0.0 all-gather.5.cloned.1.call-start
  7.2 6.1 %multiply_reduce_fusion.4 = f32[]{:T(128)} fusion(f32[4,512,1024]{2,1,0:T(8,128)} %param.17), kind=kLoop, calls=%fused_computation.25 | loop fusion | flops 4194303 | bytes 8388612 | tf_op jit(solution)/shard_map/reduce_sum | solution.py:58
  14.0 42.2 %psum.7 = f32[]{:T(128)} all-reduce(f32[]{:T(128)} %multiply_reduce_fusion.4), channel_id=1, replica_groups=mesh['dp'=8,'fsdp'=4] {'dp','fsdp'}, use_global_device_ids=true, to_apply=%region_1.0 | all-reduce | flops 1 | bytes 8 | tf_op jit(solution)/shard_map/psum | solution.py:58
  57.0 0.0 copy-start.5
  57.0 20.8 %fusion.30 = (bf16[4,512,1024]{2,1,0:T(8,128)(2,1)}, f32[4,512,1024]{2,1,0:T(8,128)}, f32[4,512,1024]{2,1,0:T(8,128)}, f32[4,512,1024]{2,1,0:T(8,128)}) fusion(f32[4,512,1024]{2,1,0:T(8,128)} %param.14, f32[4,512,1024]{2,1,0:T(8,128)} %param.17, f32[]{:T(128)S(6)} %min.3, f32[4,512,1024]{2,1,0:T(8,128)} %param.15, f32[4,512,1024]{2,1,0:T(8,128)} %param.16), kind=kLoop, calls=%fused_computation.71 | loop fusion | flops 35651584 | bytes 62914564 | tf_op jit(solution)/shard_map/convert_element_type | solution.py:61
  77.8 0.0 all-gather.5.cloned.1.call-update
  77.8 0.2 all-gather.7.cloned.1.call-start
  78.0 0.0 copy-start.3
  78.9 0.0 copy-done.5
  78.9 14.7 %multiply_sine_fusion.1 = (f32[512,1024]{1,0:T(8,128)S(1)}, f32[512,1024]{1,0:T(8,128)S(1)}, f32[512,1024]{1,0:T(8,128)S(1)}, f32[512,1024]{1,0:T(8,128)S(1)}) fusion(f32[1024]{0:T(1024)S(1)} %negate_power_fusion, f32[512]{0:T(512)S(1)} %get-tuple-element.24, f32[512]{0:T(512)S(1)} %get-tuple-element.25), kind=kLoop, calls=%fused_computation.41 | loop fusion | flops 1048576 | bytes 8396800 | tf_op jit(solution)/shard_map/sin | solution.py:24
  93.7 0.0 copy-done.3
  93.7 1.7 fusion.28
  95.4 0.0 copy-start
  95.4 0.0 copy-start.4
  95.4 3.2 copy-done
  98.6 1.0 multiply_reduce_fusion.3
  99.6 0.0 copy-done.4
  99.6 139.0 %all-gather.5.cloned.1.call-done = bf16[4,4096,1024]{2,1,0:T(8,128)(2,1)} async-done(((bf16[4,512,1024]{2,1,0:T(8,128)(2,1)}), bf16[4,4096,1024]{2,1,0:T(8,128)(2,1)}) %all-gather.5.cloned.1.call-update) | async-done | bytes 33554448 | tf_op jit(solution)/shard_map/all_gather | solution.py:67
  238.6 11.3 %fusion.18 = bf16[512,1024]{1,0:T(8,128)(2,1)} fusion(bf16[4,4096,1024]{2,1,0:T(8,128)(2,1)} %all-gather.5.cloned.1.call-done, f32[512,4096]{1,0:T(8,128)} %copy-done, f32[4096]{0:T(1024)S(1)} %bitcast.33, f32[512]{0:T(512)S(1)} %add_rsqrt_fusion.3, f32[512]{0:T(512)S(1)} %broadcast_multiply_fusion.3), kind=kOutput, calls=%fused_computation.43 | convolution fusion | flops 4303880192 | bytes 17846272 | tf_op jit(solution)/shard_map/dot_general | solution.py:70
  249.9 0.0 all-gather.7.cloned.1.call-update
  249.9 0.0 all-gather.9.cloned.1.call-start
  250.0 80.8 %all-gather.7.cloned.1.call-done = bf16[512,4096]{1,0:T(8,128)(2,1)} async-done(((bf16[512,1024]{1,0:T(8,128)(2,1)}), bf16[512,4096]{1,0:T(8,128)(2,1)}) %all-gather.7.cloned.1.call-update) | async-done | bytes 4194320 | tf_op jit(solution)/shard_map/all_gather | solution.py:50
  330.8 0.0 copy-start.2
  330.8 0.0 slice-start
  330.8 5.6 %fusion.22 = f32[512]{0:T(512)S(1)} fusion(f32[512,4096]{1,0:T(8,128)} %copy-done, bf16[512,4096]{1,0:T(8,128)(2,1)} %all-gather.7.cloned.1.call-done), kind=kLoop, calls=%fused_computation.47 | loop fusion | flops 6290944 | bytes 12584960 | tf_op jit(solution)/shard_map/reduce_sum | solution.py:29
  336.4 0.1 copy-done.2
  336.6 0.0 slice-start.1
  336.6 5.2 multiply_reduce_fusion.2
  341.8 0.0 slice-done
  341.8 0.0 slice-done.1
  341.8 9.2 %fusion.19 = bf16[512,1024]{1,0:T(8,128)(2,1)} fusion(bf16[4,4096,1024]{2,1,0:T(8,128)(2,1)} %all-gather.5.cloned.1.call-done, f32[4096]{0:T(1024)S(1)} %bitcast.32, f32[512]{0:T(512)S(1)} %add_rsqrt_fusion.2, f32[512]{0:T(512)S(1)} %broadcast_multiply_fusion.2, f32[512,4096]{1,0:T(8,128)S(1)} %bitcast.29, bf16[512,4096]{1,0:T(8,128)(2,1)S(1)} %copy-done.2), kind=kOutput, calls=%fused_computation.44 | convolution fusion | flops 4308074496 | bytes 22040576 | tf_op jit(solution)/shard_map/dot_general | solution.py:70
  351.0 0.0 all-gather.9.cloned.1.call-update
  351.1 0.3 all-gather.11.cloned.1.call-start
  351.4 79.1 %all-gather.9.cloned.1.call-done = bf16[512,4096]{1,0:T(8,128)(2,1)} async-done(((bf16[512,1024]{1,0:T(8,128)(2,1)}), bf16[512,4096]{1,0:T(8,128)(2,1)}) %all-gather.9.cloned.1.call-update) | async-done | bytes 4194320 | tf_op jit(solution)/shard_map/all_gather | solution.py:50
  430.4 10.3 %fusion.27 = (f32[512]{0:T(512)S(1)}, f32[512,4096]{1,0:T(8,128)}) fusion(bf16[512,4096]{1,0:T(8,128)(2,1)} %all-gather.9.cloned.1.call-done, f32[512,4096]{1,0:T(8,128)} %copy-done, bf16[512,4096]{1,0:T(8,128)(2,1)} %all-gather.7.cloned.1.call-done), kind=kLoop, calls=%fused_computation.69 | loop fusion | flops 10485248 | bytes 25167872 | tf_op jit(solution)/shard_map/reduce_sum | solution.py:29
  440.7 0.0 copy-start.1
  440.8 4.5 multiply_reduce_fusion.1
  445.3 1.3 copy-done.1
  446.5 9.0 %fusion.20 = bf16[512,1024]{1,0:T(8,128)(2,1)} fusion(bf16[4,4096,1024]{2,1,0:T(8,128)(2,1)} %all-gather.5.cloned.1.call-done, f32[512,4096]{1,0:T(8,128)S(1)} %copy-done.1, f32[4096]{0:T(1024)S(1)} %bitcast.31, f32[512]{0:T(512)S(1)} %add_rsqrt_fusion.1, f32[512]{0:T(512)S(1)} %broadcast_multiply_fusion.1), kind=kOutput, calls=%fused_computation.45 | convolution fusion | flops 4303880192 | bytes 17846272 | tf_op jit(solution)/shard_map/dot_general | solution.py:70
  455.6 0.0 all-gather.11.cloned.1.call-update
  455.6 79.4 %all-gather.11.cloned.1.call-done = bf16[512,4096]{1,0:T(8,128)(2,1)} async-done(((bf16[512,1024]{1,0:T(8,128)(2,1)}), bf16[512,4096]{1,0:T(8,128)(2,1)}) %all-gather.11.cloned.1.call-update) | async-done | bytes 4194320 | tf_op jit(solution)/shard_map/all_gather | solution.py:50
  535.0 5.5 fusion.26
  540.5 1.0 multiply_reduce_fusion
  541.4 8.9 %select_convert_fusion = bf16[512,1024]{1,0:T(8,128)(2,1)} fusion(f32[512,4096]{1,0:T(8,128)S(1)} %get-tuple-element.5, s32[]{:T(128)S(6)} %select_n.26, bf16[4,4096,1024]{2,1,0:T(8,128)(2,1)} %all-gather.5.cloned.1.call-done, f32[4096]{0:T(1024)S(1)} %bitcast.30, f32[512]{0:T(512)S(1)} %add_rsqrt_fusion, f32[512]{0:T(512)S(1)} %broadcast_multiply_fusion, ...), kind=kOutput, calls=%fused_computation.42 | convolution fusion | flops 4305977344 | bytes 19943940 | tf_op jit(solution)/shard_map/dot_general | solution.py:70
  (13 shorter events, 0.1 us)
Async XLA Ops:
  7.2 231.5 %all-gather.5.cloned.1.call-start = ((), (), s32[]{:S(2)}) async-start(), calls=%async_computation | async-start | bytes 37748736 | tf_op jit(solution)/shard_map/all_gather | solution.py:67
  57.0 21.9 %copy-start.5 = (s32[512]{0:T(512)S(1)}, s32[512]{0:T(512)}, u32[]{:S(2)}) copy-start(s32[512]{0:T(512)} %param.11) | copy-start | bytes 6148
  77.8 253.0 %all-gather.7.cloned.1.call-start = ((), (), s32[]{:S(2)}) async-start(), calls=%async_computation.1 | async-start | bytes 5242880 | tf_op jit(solution)/shard_map/all_gather | solution.py:50
  78.0 15.6 %copy-start.3 = (bf16[512,4096]{1,0:T(8,128)(2,1)S(1)}, bf16[512,4096]{1,0:T(8,128)(2,1)}, u32[]{:S(2)}) copy-start(bf16[512,4096]{1,0:T(8,128)(2,1)} %param.9) | copy-start | bytes 12582916
  95.4 3.2 copy-start
  95.4 4.2 copy-start.4
  249.9 180.5 %all-gather.9.cloned.1.call-start = ((), (), s32[]{:S(2)}) async-start(), calls=%async_computation.2 | async-start | bytes 5242880 | tf_op jit(solution)/shard_map/all_gather | solution.py:50
  330.8 5.8 %copy-start.2 = (bf16[512,4096]{1,0:T(8,128)(2,1)S(1)}, bf16[512,4096]{1,0:T(8,128)(2,1)}, u32[]{:S(2)}) copy-start(bf16[512,4096]{1,0:T(8,128)(2,1)} %all-gather.7.cloned.1.call-done) | copy-start | bytes 12582916
  330.8 11.0 %slice-start = ((s8[8388608]{0:T(1024)(128)(4,1)}), s8[4194304]{0:T(1024)(128)(4,1)S(1)}, s32[]{:S(2)}) async-start(s8[8388608]{0:T(1024)(128)(4,1)} %bitcast.28), calls=%async_computation.4 | async-start | bytes 8388608
  336.6 5.2 slice-start.1
  351.1 183.9 %all-gather.11.cloned.1.call-start = ((), (), s32[]{:S(2)}) async-start(), calls=%async_computation.3 | async-start | bytes 5242880 | tf_op jit(solution)/shard_map/all_gather | solution.py:50
  440.7 5.8 %copy-start.1 = (f32[512,4096]{1,0:T(8,128)S(1)}, f32[512,4096]{1,0:T(8,128)}, u32[]{:S(2)}) copy-start(f32[512,4096]{1,0:T(8,128)} %get-tuple-element.7) | copy-start | bytes 25165828
Sparse Core Ops, SparseCore 0:
  77.9 160.6 all-gather.4
  250.0 80.7 all-gather.6
  351.2 79.2 all-gather.8
  455.7 79.2 all-gather.10
where the time goes:
time: 557 us
  waiting for transfers between devices  378 us (68%)
  other arithmetic  76.5 us (14%)
  blocking collectives  42.2 us (8%)
  matrix products  38.4 us (7%)
  between operations  16.1 us (3%)
    all_gather x3, waiting for transfers between devices, advance(): widened = lax.all_gather(branch, 'fsdp', axis=1, tiled=True)  239 us
    all_gather x1, waiting for transfers between devices, per_device(): gathered = lax.all_gather(weights, 'dp', axis=1, tiled=True)  139 us
    psum x1, blocking collectives, per_device(): squares = lax.psum(jnp.sum(gradients * gradients), ('dp', 'fsdp'))  42.2 us
    dot_general x4, matrix products, per_device(): jnp.dot(normed, gathered[current], preferred_element_type=jnp.float32)  38.4 us
    reduce_sum x4, other arithmetic, layer_norm(): centre = jnp.mean(stream, axis=1, keepdims=True)  23.1 us
    convert_element_type x1, other arithmetic, per_device(): weights = params_new.astype(jnp.bfloat16)  20.8 us
    sin x1, other arithmetic, position_code(): jnp.sin(across)  14.7 us
    reduce_sum x4, other arithmetic, layer_norm(): spread = jnp.mean(shifted * shifted, axis=1, keepdims=True)  11.6 us
  transfers between devices with their start and end apart: 4, of which 4 were waited for; matrix products, arithmetic and copies ran while one was open for 3% of the time, Pallas kernels for 0%

commit v1 on v0

--- a/solution.py
+++ b/solution.py
@@ -47,7 +47,7 @@
 
 def advance(stream, branch, current, col_first, col_count):
     if current + 1 < LAYERS:
-        widened = lax.all_gather(branch, "fsdp", axis=1, tiled=True)
+        widened = jnp.concatenate(lax.all_gather(branch, "fsdp"), axis=1)
         return stream + widened.astype(jnp.float32)
     return lax.dynamic_slice_in_dim(stream, col_first, col_count, 1) + branch.astype(jnp.float32)
 

time: 557 us -> 596 us (1.070)
  other arithmetic: 76.5 us -> 96.9 us
  local copies, waits for them, and re-layouts: 4.64 us -> 19.2 us
    convert_element_type x0 -> x3, local copies, waits for them, and re-layouts: none -> 12.1 us  [advance(): return stream + widened.astype(jnp.float32)]
    unnamed x1 -> x3, other arithmetic: 0.01 us -> 9.64 us
    reduce_sum x4, other arithmetic: 23.1 us -> 31 us  [layer_norm(): centre = jnp.mean(stream, axis=1, keepdims=True)]
where the time goes in v1:
time: 596 us; the launch traced here: 592 us
  waiting for transfers between devices  378 us (63%)
  other arithmetic  96.9 us (16%)
  blocking collectives  42.2 us (7%)
  matrix products  38.5 us (6%)
  local copies, waits for them, and re-layouts  19.2 us (3%)
  between operations  16.3 us (3%)
    all_gather x3, waiting for transfers between devices, advance(): widened = jnp.concatenate(lax.all_gather(branch, 'fsdp'), axis=1)  239 us
    all_gather x1, waiting for transfers between devices, per_device(): gathered = lax.all_gather(weights, 'dp', axis=1, tiled=True)  139 us
    psum x1, blocking collectives, per_device(): squares = lax.psum(jnp.sum(gradients * gradients), ('dp', 'fsdp'))  42.2 us
    dot_general x4, matrix products, per_device(): jnp.dot(normed, gathered[current], preferred_element_type=jnp.float32)  38.5 us
    reduce_sum x4, other arithmetic, layer_norm(): centre = jnp.mean(stream, axis=1, keepdims=True)  31 us
    convert_element_type x1, other arithmetic, per_device(): weights = params_new.astype(jnp.bfloat16)  20.9 us
    sin x1, other arithmetic, position_code(): jnp.sin(across)  14.7 us
    reduce_sum x4, other arithmetic, layer_norm(): spread = jnp.mean(shifted * shifted, axis=1, keepdims=True)  14.4 us
  transfers between devices with their start and end apart: 4, of which 4 were waited for; matrix products, arithmetic and copies ran while one was open for 3% of the time, Pallas kernels for 0%

profile of v1, /device:TPU:0, one launch (start us, length us, event | category | flops | bytes accessed | tf_op | source)
XLA Modules:
  0.0 592.1 jit_solution(1253583413773540594)
XLA Ops:
  7.2 0.0 all-gather.8.cloned.1.call-start
  7.2 6.1 %multiply_reduce_fusion.4 = f32[]{:T(128)} fusion(f32[4,512,1024]{2,1,0:T(8,128)} %param.17), kind=kLoop, calls=%fused_computation.25 | loop fusion | flops 4194303 | bytes 8388612 | tf_op jit(solution)/shard_map/reduce_sum | solution.py:58
  14.0 42.2 %psum.7 = f32[]{:T(128)} all-reduce(f32[]{:T(128)} %multiply_reduce_fusion.4), channel_id=1, replica_groups=mesh['dp'=8,'fsdp'=4] {'dp','fsdp'}, use_global_device_ids=true, to_apply=%region_1.0 | all-reduce | flops 1 | bytes 8 | tf_op jit(solution)/shard_map/psum | solution.py:58
  57.0 0.0 copy-start.6
  57.0 20.9 %fusion.30 = (bf16[4,512,1024]{2,1,0:T(8,128)(2,1)}, f32[4,512,1024]{2,1,0:T(8,128)}, f32[4,512,1024]{2,1,0:T(8,128)}, f32[4,512,1024]{2,1,0:T(8,128)}) fusion(f32[4,512,1024]{2,1,0:T(8,128)} %param.14, f32[4,512,1024]{2,1,0:T(8,128)} %param.17, f32[]{:T(128)S(6)} %min.3, f32[4,512,1024]{2,1,0:T(8,128)} %param.15, f32[4,512,1024]{2,1,0:T(8,128)} %param.16), kind=kLoop, calls=%fused_computation.71 | loop fusion | flops 35651584 | bytes 62914564 | tf_op jit(solution)/shard_map/convert_element_type | solution.py:61
  77.8 0.0 all-gather.8.cloned.1.call-update
  77.9 0.5 all-gather.10.cloned.1.call-start
  78.4 0.0 copy-start.4
  79.2 0.0 copy-done.6
  79.2 14.7 %multiply_sine_fusion.1 = (f32[512,1024]{1,0:T(8,128)S(1)}, f32[512,1024]{1,0:T(8,128)S(1)}, f32[512,1024]{1,0:T(8,128)S(1)}, f32[512,1024]{1,0:T(8,128)S(1)}) fusion(f32[1024]{0:T(1024)S(1)} %negate_power_fusion, f32[512]{0:T(512)S(1)} %get-tuple-element.26, f32[512]{0:T(512)S(1)} %get-tuple-element.27), kind=kLoop, calls=%fused_computation.41 | loop fusion | flops 1048576 | bytes 8396800 | tf_op jit(solution)/shard_map/sin | solution.py:24
  94.0 0.0 copy-done.4
  94.0 1.7 fusion.28
  95.7 0.0 copy-start.1
  95.7 0.0 copy-start.5
  95.7 3.2 copy-done.1
  98.9 1.0 multiply_reduce_fusion.3
  99.9 0.0 copy-done.5
  99.9 138.8 %all-gather.8.cloned.1.call-done = bf16[4,4096,1024]{2,1,0:T(8,128)(2,1)} async-done(((bf16[4,512,1024]{2,1,0:T(8,128)(2,1)}), bf16[4,4096,1024]{2,1,0:T(8,128)(2,1)}) %all-gather.8.cloned.1.call-update) | async-done | bytes 33554448 | tf_op jit(solution)/shard_map/all_gather | solution.py:67
  238.7 11.3 %fusion.18 = bf16[512,1024]{1,0:T(8,128)(2,1)} fusion(bf16[4,4096,1024]{2,1,0:T(8,128)(2,1)} %all-gather.8.cloned.1.call-done, f32[512,4096]{1,0:T(8,128)} %copy-done.1, f32[4096]{0:T(1024)S(1)} %bitcast.55, f32[512]{0:T(512)S(1)} %add_rsqrt_fusion.3, f32[512]{0:T(512)S(1)} %broadcast_multiply_fusion.3), kind=kOutput, calls=%fused_computation.43 | convolution fusion | flops 4303880192 | bytes 17846272 | tf_op jit(solution)/shard_map/dot_general | solution.py:70
  250.0 0.0 all-gather.10.cloned.1.call-update
  250.0 0.0 all-gather.12.cloned.1.call-start
  250.0 80.8 %all-gather.10.cloned.1.call-done = bf16[2048,1024]{1,0:T(8,128)(2,1)} async-done(((bf16[512,1024]{1,0:T(8,128)(2,1)}), bf16[2048,1024]{1,0:T(8,128)(2,1)}) %all-gather.10.cloned.1.call-update) | async-done | bytes 4194320 | tf_op jit(solution)/shard_map/all_gather | solution.py:50
  330.9 3.2 convert_bitcast_fusion.2
  334.1 4.1 copy.16
  338.2 9.8 %fusion.27 = (f32[512]{0:T(512)S(1)}, f32[512,4096]{1,0:T(8,128)}) fusion(f32[512,4096]{1,0:T(8,128)} %copy-done.1, f32[512,4096]{1,0:T(8,128)} %bitcast.46), kind=kLoop, calls=%fused_computation.69 | loop fusion | flops 4193792 | bytes 25167872 | tf_op jit(solution)/shard_map/reduce_sum | solution.py:29
  347.9 0.0 copy-start.2
  347.9 4.5 multiply_reduce_fusion.2
  352.4 1.3 copy-done.2
  353.7 9.1 %fusion.19 = bf16[512,1024]{1,0:T(8,128)(2,1)} fusion(bf16[4,4096,1024]{2,1,0:T(8,128)(2,1)} %all-gather.8.cloned.1.call-done, f32[512,4096]{1,0:T(8,128)S(1)} %copy-done.2, f32[4096]{0:T(1024)S(1)} %bitcast.54, f32[512]{0:T(512)S(1)} %add_rsqrt_fusion.2, f32[512]{0:T(512)S(1)} %broadcast_multiply_fusion.2), kind=kOutput, calls=%fused_computation.44 | convolution fusion | flops 4303880192 | bytes 17846272 | tf_op jit(solution)/shard_map/dot_general | solution.py:70
  362.8 0.0 all-gather.12.cloned.1.call-update
  362.8 0.3 all-gather.14.cloned.1.call-start
  363.0 79.1 %all-gather.12.cloned.1.call-done = bf16[2048,1024]{1,0:T(8,128)(2,1)} async-done(((bf16[512,1024]{1,0:T(8,128)(2,1)}), bf16[2048,1024]{1,0:T(8,128)(2,1)}) %all-gather.12.cloned.1.call-update) | async-done | bytes 4194320 | tf_op jit(solution)/shard_map/all_gather | solution.py:50
  442.2 3.2 convert_bitcast_fusion.1
  445.4 4.1 copy.17
  449.4 9.8 %fusion.26 = (f32[512]{0:T(512)S(1)}, f32[512,4096]{1,0:T(8,128)}) fusion(f32[512,4096]{1,0:T(8,128)} %get-tuple-element.9, f32[512,4096]{1,0:T(8,128)} %bitcast.47), kind=kLoop, calls=%fused_computation.68 | loop fusion | flops 4193792 | bytes 25167872 | tf_op jit(solution)/shard_map/reduce_sum | solution.py:29
  459.2 0.0 copy-start
  459.2 4.5 multiply_reduce_fusion.1
  463.7 1.3 copy-done
  465.0 9.1 %fusion.20 = bf16[512,1024]{1,0:T(8,128)(2,1)} fusion(bf16[4,4096,1024]{2,1,0:T(8,128)(2,1)} %all-gather.8.cloned.1.call-done, f32[512,4096]{1,0:T(8,128)S(1)} %copy-done, f32[4096]{0:T(1024)S(1)} %bitcast.53, f32[512]{0:T(512)S(1)} %add_rsqrt_fusion.1, f32[512]{0:T(512)S(1)} %broadcast_multiply_fusion.1), kind=kOutput, calls=%fused_computation.45 | convolution fusion | flops 4303880192 | bytes 17846272 | tf_op jit(solution)/shard_map/dot_general | solution.py:70
  474.0 0.0 all-gather.14.cloned.1.call-update
  474.1 79.4 %all-gather.14.cloned.1.call-done = bf16[2048,1024]{1,0:T(8,128)(2,1)} async-done(((bf16[512,1024]{1,0:T(8,128)(2,1)}), bf16[2048,1024]{1,0:T(8,128)(2,1)}) %all-gather.14.cloned.1.call-update) | async-done | bytes 4194320 | tf_op jit(solution)/shard_map/all_gather | solution.py:50
  553.4 3.2 convert_bitcast_fusion
  556.7 4.0 copy.18
  560.7 9.8 %fusion.25 = (f32[512]{0:T(512)S(1)}, f32[512,4096]{1,0:T(8,128)}) fusion(f32[512,4096]{1,0:T(8,128)} %get-tuple-element.7, f32[512,4096]{1,0:T(8,128)} %bitcast.48), kind=kLoop, calls=%fused_computation.67 | loop fusion | flops 4193792 | bytes 25167872 | tf_op jit(solution)/shard_map/reduce_sum | solution.py:29
  570.5 0.0 copy-start.3
  570.5 4.5 multiply_reduce_fusion
  575.0 1.3 copy-done.3
  576.3 9.1 %select_convert_fusion = bf16[512,1024]{1,0:T(8,128)(2,1)} fusion(f32[512,4096]{1,0:T(8,128)S(1)} %copy-done.3, s32[]{:T(128)S(6)} %select_n.26, bf16[4,4096,1024]{2,1,0:T(8,128)(2,1)} %all-gather.8.cloned.1.call-done, f32[4096]{0:T(1024)S(1)} %bitcast.52, f32[512]{0:T(512)S(1)} %add_rsqrt_fusion, f32[512]{0:T(512)S(1)} %broadcast_multiply_fusion, ...), kind=kOutput, calls=%fused_computation.42 | convolution fusion | flops 4305977344 | bytes 19943940 | tf_op jit(solution)/shard_map/dot_general | solution.py:70
  (12 shorter events, 0.1 us)
Async XLA Ops:
  7.2 231.5 %all-gather.8.cloned.1.call-start = ((), (), s32[]{:S(2)}) async-start(), calls=%async_computation | async-start | bytes 37748736 | tf_op jit(solution)/shard_map/all_gather | solution.py:67
  57.0 22.2 %copy-start.6 = (s32[512]{0:T(512)S(1)}, s32[512]{0:T(512)}, u32[]{:S(2)}) copy-start(s32[512]{0:T(512)} %param.11) | copy-start | bytes 6148
  77.9 253.0 %all-gather.10.cloned.1.call-start = ((), (), s32[]{:S(2)}) async-start(), calls=%async_computation.1 | async-start | bytes 5242880 | tf_op jit(solution)/shard_map/all_gather | solution.py:50
  78.4 15.6 %copy-start.4 = (bf16[512,4096]{1,0:T(8,128)(2,1)S(1)}, bf16[512,4096]{1,0:T(8,128)(2,1)}, u32[]{:S(2)}) copy-start(bf16[512,4096]{1,0:T(8,128)(2,1)} %param.9) | copy-start | bytes 12582916
  95.7 3.2 copy-start.1
  95.7 4.2 copy-start.5
  250.0 192.2 %all-gather.12.cloned.1.call-start = ((), (), s32[]{:S(2)}) async-start(), calls=%async_computation.2 | async-start | bytes 5242880 | tf_op jit(solution)/shard_map/all_gather | solution.py:50
  347.9 5.8 copy-start.2
  362.8 190.7 %all-gather.14.cloned.1.call-start = ((), (), s32[]{:S(2)}) async-start(), calls=%async_computation.3 | async-start | bytes 5242880 | tf_op jit(solution)/shard_map/all_gather | solution.py:50
  459.2 5.8 copy-start
  570.5 5.8 copy-start.3
Sparse Core Ops, SparseCore 0:
  78.0 160.6 all-gather.7
  250.1 80.7 all-gather.9
  362.9 79.2 all-gather.11
  474.2 79.2 all-gather.13
